TPU v7x, 32 devices: a whole 2x2x4 slice. The times are simulated.
32 devices in a mesh: row: 4 (over y, core), col: 8 (over z, x).
Axes of the slice: x: 2, y: 2, z: 4, core: 2. Of those that a mesh axis runs over, the one named last changes fastest.
Arguments:
- l_saved: bfloat16 [16, 4, 256, 8, 256], P(None, 'row', None, 'col'), as said below
- l_grad: bfloat16 [16, 4, 256, 8, 256], P(None, 'row', None, 'col'), as said below
Outputs:
- grad_out: float32 [16, 4, 256, 8, 256], P(None, 'row', None, 'col')
Inputs may be any that keep to these rules, and one draw needn't show every extreme that they name: Read as one matrix of 16384 rows, l_saved is lower triangular with its diagonal between 1 and 2. Read as one matrix, l_grad is zero above the diagonal.
All inputs are finite; a program needn't handle non-finite values.
Results may differ from a plain program's by a relative error of at most 0.0003.
Values may be sent and summed in bfloat16 or wider, within the bound.
A program may use at most 64 MiB of HBM per device.

v0:
```python
import jax
import jax.numpy as jnp
from jax import lax
from jax.sharding import PartitionSpec as P

HIGH = lax.Precision.HIGHEST


def from_root(array, axis, root):
    mine = lax.axis_index(axis) == root
    return lax.psum(jnp.where(mine, array, jnp.zeros_like(array)), axis)


def right_solve(factor, rhs):
    return lax.linalg.triangular_solve(factor, rhs, left_side=False, lower=True)


def diag_gradient(factor, lower_part):
    eye = jnp.eye(factor.shape[0], dtype=jnp.float32)
    middle = jnp.dot(factor.T, lower_part, precision=HIGH, preferred_element_type=jnp.float32)
    middle = jnp.tril(middle) - 0.5 * middle * eye
    half = lax.linalg.triangular_solve(factor, middle, left_side=True, lower=True, transpose_a=True)
    full = right_solve(factor, half)
    return full + full.T


def stacked_inner(left, right):
    flat_left = left.reshape(-1, left.shape[-1])
    flat_right = right.reshape(-1, right.shape[-1]).astype(jnp.float32)
    return lax.dot_general(
        flat_left,
        flat_right,
        (((0,), (0,)), ((), ())),
        precision=HIGH,
        preferred_element_type=jnp.float32,
    )


def solve_rows(diag_factor, column, below):
    rows_here, tile = (column.shape[0], column.shape[1])
    inverse = right_solve(diag_factor, jnp.eye(tile, dtype=jnp.float32))
    solved = jnp.dot(
        column.reshape(-1, tile), inverse, precision=HIGH, preferred_element_type=jnp.float32
    ).reshape(rows_here, tile, tile)
    return jnp.where(below, solved, jnp.float32(0.0))


def diag_down(piece, owner_row):
    return from_root(piece, "row", owner_row).astype(jnp.float32)


def per_device(l_saved, l_grad):
    rows_here = l_saved.shape[0]
    tile = l_saved.shape[2]
    n_row = lax.axis_size("row")
    n_col = lax.axis_size("col")
    factor = l_saved.reshape(rows_here, tile, tile)
    grad = l_grad.reshape(rows_here, tile, tile).astype(jnp.float32)
    my_row = lax.axis_index("row")
    my_col = lax.axis_index("col")
    tile_rows = jnp.arange(rows_here, dtype=jnp.int32) * n_row + my_row
    eye = jnp.eye(tile, dtype=jnp.float32)
    for panel in (n_col - 1, n_col - 2):
        owner_row = panel % n_row
        local = panel // n_row
        at_owner = my_row == owner_row
        below = (tile_rows > panel)[:, None, None]
        diag_factor = diag_down(factor[local], owner_row)
        cbar = solve_rows(diag_factor, grad, below)
        term = jnp.where(at_owner, grad[local], jnp.float32(0.0)) - stacked_inner(cbar, factor)
        total = lax.psum(term, "row")
        sym = diag_gradient(diag_factor, jnp.tril(total))
        sent = from_root(jnp.concatenate([cbar, sym[None]], 0), "col", panel)
        cbar = sent[:rows_here]
        sym = sent[rows_here]
        row_factor = from_root(factor[local], "row", owner_row).astype(jnp.float32)
        update = jnp.dot(
            cbar.reshape(-1, tile), row_factor, precision=HIGH, preferred_element_type=jnp.float32
        )
        partial_sum = stacked_inner(cbar, factor)
        summed = lax.psum(partial_sum, "row")
        own_row = grad[local] - (
            summed + jnp.dot(sym, row_factor, precision=HIGH, preferred_element_type=jnp.float32)
        )
        updated = grad - update.reshape(rows_here, tile, tile)
        updated = updated.at[local].set(jnp.where(at_owner, own_row, updated[local]))
        abar = jnp.tril(sym) - 0.5 * sym * eye
        panel_col = jnp.where(
            below,
            cbar,
            jnp.where((tile_rows == panel)[:, None, None], abar[None], jnp.float32(0.0)),
        )
        grad = jnp.where(my_col < panel, updated, jnp.where(my_col == panel, panel_col, grad))
    return grad.reshape(l_grad.shape)


def solution(mesh):
    in_specs = (P(None, "row", None, "col", None), P(None, "row", None, "col", None))
    out_specs = P(None, "row", None, "col", None)
    return jax.shard_map(
        per_device, mesh=mesh, in_specs=in_specs, out_specs=out_specs, check_vma=False
    )
```

profile of v0, /device:TPU:0, one launch (start us, length us, event | category | flops | bytes accessed | tf_op | source)
XLA Modules:
  0.0 607.6 jit_solution(4179768059537039904)
XLA Ops:
  8.3 4.3 convert_element_type.13
  12.6 32.2 %all-reduce.21.cloned.1.call-done = (bf16[256,256]{1,0:T(8,128)(2,1)}, bf16[256,256]{1,0:T(8,128)(2,1)}) async-done(((bf16[256,256]{1,0:T(8,128)(2,1)}, bf16[256,256]{1,0:T(8,128)(2,1)}), (bf16[256,256]{1,0:T(8,128)(2,1)}, bf16[256,256]{1,0:T(8,128)(2,1)})) %all-reduce.21.cloned.1.call-update) | async-done | bytes 262160 | tf_op jit(solution)/shard_map/psum | solution.py:11
  50.1 19.7 %custom-call.10 = f32[2,128,128]{1,2,0:T(8,128)S(1)} custom-call(f32[2,128,128]{2,1,0:T(8,128)S(1)} %get-tuple-element.71), custom_call_target="InvertDiagBlocksLowerTriangular" | custom-call | tf_op jit(solution)/shard_map/triangular_solve/custom-call.1 | solution.py:15
  74.6 5.8 copy.9
  80.3 5.0 fusion.5
  85.4 4.7 broadcast_select_fusion
  90.2 27.7 %all-reduce.9.cloned.1.call-done = f32[256,256]{1,0:T(8,128)} async-done(((f32[256,256]{1,0:T(8,128)}), f32[256,256]{1,0:T(8,128)}) %all-reduce.9.cloned.1.call-update) | async-done | bytes 262160 | tf_op jit(solution)/shard_map/psum | solution.py:71
  122.8 4.7 maximum_select_fusion
  127.5 13.2 %all-reduce.13.cloned.1.call-start = ((), (), s32[]{:S(2)}) async-start(), calls=%async_computation.2 | async-start | bytes 524288 | tf_op jit(solution)/shard_map/psum | solution.py:81
  144.7 19.7 %custom-call.13 = f32[2,128,128]{1,2,0:T(8,128)S(1)} custom-call(f32[2,128,128]{2,1,0:T(8,128)S(1)} %get-tuple-element.74), custom_call_target="InvertDiagBlocksLowerTriangular" | custom-call | tf_op jit(solution)/shard_map/triangular_solve/custom-call.1 | solution.py:15
  165.3 125.3 %all-reduce.11.cloned.1.call-done = f32[17,256,256]{2,1,0:T(8,128)} async-done(((f32[17,256,256]{2,1,0:T(8,128)}), f32[17,256,256]{2,1,0:T(8,128)}) %all-reduce.11.cloned.1.call-update) | async-done | bytes 4456464 | tf_op jit(solution)/shard_map/psum | solution.py:11
  292.9 4.1 fusion.83
  297.1 4.9 bitcast_subtract_fusion
  305.0 23.4 %all-reduce.13.cloned.1.call-done = f32[256,256]{1,0:T(8,128)} async-done(((f32[256,256]{1,0:T(8,128)}), f32[256,256]{1,0:T(8,128)}) %all-reduce.13.cloned.1.call-update) | async-done | bytes 262160 | tf_op jit(solution)/shard_map/psum | solution.py:81
  330.5 5.1 fusion
  341.3 4.2 convolution_subtract_fusion.1
  345.6 31.5 %all-reduce.15.cloned.1.call-done = f32[256,256]{1,0:T(8,128)} async-done(((f32[256,256]{1,0:T(8,128)}), f32[256,256]{1,0:T(8,128)}) %all-reduce.15.cloned.1.call-update) | async-done | bytes 262160 | tf_op jit(solution)/shard_map/psum | solution.py:71
  380.3 4.7 maximum_select_fusion.1
  385.3 162.9 %all-reduce.17.cloned.1.call-done = f32[17,256,256]{2,1,0:T(8,128)} async-done(((f32[17,256,256]{2,1,0:T(8,128)}), f32[17,256,256]{2,1,0:T(8,128)}) %all-reduce.17.cloned.1.call-update) | async-done | bytes 4456464 | tf_op jit(solution)/shard_map/psum | solution.py:11
  550.4 4.1 fusion.84
  554.6 5.6 convolution_subtract_fusion
  562.3 23.7 %all-reduce.19.cloned.1.call-done = f32[256,256]{1,0:T(8,128)} async-done(((f32[256,256]{1,0:T(8,128)}), f32[256,256]{1,0:T(8,128)}) %all-reduce.19.cloned.1.call-update) | async-done | bytes 262160 | tf_op jit(solution)/shard_map/psum | solution.py:81
  588.1 5.9 select_bitcast_fusion
  594.0 6.3 %copy.7 = f32[16,1,256,1,256]{4,3,2,1,0:T(1,128)} copy(f32[16,1,256,1,256]{4,2,0,3,1:T(8,128)S(1)} %select_bitcast_fusion) | data formatting | bytes 8388608 | tf_op jit(solution)/shard_map/reshape | solution.py:94
  (98 shorter events, 52.5 us)
Async XLA Ops:
  6.5 38.3 %all-reduce.21.cloned.1.call-start = ((), (), s32[]{:S(2)}) async-start(), calls=%async_computation.6 | async-start | bytes 524288 | tf_op jit(solution)/shard_map/psum | solution.py:11
  8.2 109.7 %all-reduce.9.cloned.1.call-start = ((), (), s32[]{:S(2)}) async-start(), calls=%async_computation | async-start | bytes 524288 | tf_op jit(solution)/shard_map/psum | solution.py:71
  8.3 62.4 %copy-start.3 = (bf16[16,1,256,1,256]{4,2,3,1,0:T(8,128)(2,1)S(1)}, bf16[16,1,256,1,256]{4,2,3,1,0:T(8,128)(2,1)}, u32[]{:S(2)}) copy-start(bf16[16,1,256,1,256]{4,2,3,1,0:T(8,128)(2,1)} %param.11) | copy-start | bytes 6291460
  74.6 5.8 copy-start.2
  85.4 205.3 %all-reduce.11.cloned.1.call-start = ((), (), s32[]{:S(2)}) async-start(), calls=%async_computation.1 | async-start | bytes 8912896 | tf_op jit(solution)/shard_map/psum | solution.py:11
  85.4 32.4 %copy-start.7 = (bf16[256,256]{1,0:T(8,128)(2,1)S(1)}, bf16[256,256]{1,0:T(8,128)(2,1)}, u32[]{:S(2)}) copy-start(bf16[256,256]{1,0:T(8,128)(2,1)} %get-tuple-element.93) | copy-start | bytes 393220
  127.5 201.0 %all-reduce.13.cloned.1.call-start = ((), (), s32[]{:S(2)}) async-start(), calls=%async_computation.2 | async-start | bytes 524288 | tf_op jit(solution)/shard_map/psum | solution.py:81
  290.7 2.2 slice-start.3
  297.0 80.1 %all-reduce.15.cloned.1.call-start = ((), (), s32[]{:S(2)}) async-start(), calls=%async_computation.3 | async-start | bytes 524288 | tf_op jit(solution)/shard_map/psum | solution.py:71
  302.0 2.0 copy-start.5
  335.6 3.8 copy-start
  339.4 1.9 copy-start.1
  339.4 37.7 %copy-start.6 = (bf16[256,256]{1,0:T(8,128)(2,1)S(1)}, bf16[256,256]{1,0:T(8,128)(2,1)}, u32[]{:S(2)}) copy-start(bf16[256,256]{1,0:T(8,128)(2,1)} %get-tuple-element.94) | copy-start | bytes 393220
  345.5 202.7 %all-reduce.17.cloned.1.call-start = ((), (), s32[]{:S(2)}) async-start(), calls=%async_computation.4 | async-start | bytes 8912896 | tf_op jit(solution)/shard_map/psum | solution.py:11
  385.1 201.0 %all-reduce.19.cloned.1.call-start = ((), (), s32[]{:S(2)}) async-start(), calls=%async_computation.5 | async-start | bytes 524288 | tf_op jit(solution)/shard_map/psum | solution.py:81
  548.2 2.2 slice-start.2
  550.4 11.8 %slice-start = ((s8[4456448]{0:T(1024)(128)(4,1)}), s8[262144]{0:T(1024)(128)(4,1)S(1)}, s32[]{:S(2)}) async-start(s8[4456448]{0:T(1024)(128)(4,1)} %bitcast.165), calls=%async_computation.7 | async-start | bytes 524288
  554.6 7.7 %slice-start.1 = ((s8[4456448]{0:T(1024)(128)(4,1)}), s8[4194304]{0:T(1024)(128)(4,1)S(1)}, s32[]{:S(2)}) async-start(s8[4456448]{0:T(1024)(128)(4,1)} %bitcast.165), calls=%async_computation.8 | async-start | bytes 8388608
  560.2 2.0 copy-start.4
Sparse Core Ops, SparseCore 0:
  9.7 35.0 all-reduce.20
  85.5 32.3 all-reduce.8
  127.6 163.0 all-reduce.10
  297.1 31.2 all-reduce.12
  345.7 31.3 all-reduce.14
  385.2 163.0 all-reduce.16
  554.7 31.2 all-reduce.18
where the time goes:
time: 616 us; the launch traced here: 608 us
  waiting for transfers between devices  427 us (69%)
  other arithmetic  73.2 us (12%)
  matrix products  47.7 us (8%)
  local copies, waits for them, and re-layouts  31.8 us (5%)
  between operations  14.3 us (2%)
  starting transfers between devices  13.6 us (2%)
    psum x3, waiting for transfers between devices, from_root(): return lax.psum(jnp.where(mine, array, jnp.zeros_like(array)), axis)  320 us
    psum x2, waiting for transfers between devices, per_device(): total = lax.psum(term, 'row')  59.2 us
    psum x2, waiting for transfers between devices, per_device(): summed = lax.psum(partial_sum, 'row')  47.1 us
    another operation x6, other arithmetic, right_solve(): return lax.linalg.triangular_solve(factor, rhs, left_side=False, lower=True)  41.1 us
    dot_general x4, matrix products, stacked_inner(): lax.dot_general(flat_left, flat_right, (((0,), (0,)), ((), ())), precisio...  17.4 us
    psum x2, starting transfers between devices, per_device(): summed = lax.psum(partial_sum, 'row')  13.4 us
  transfers between devices with their start and end apart: 7, of which 7 were waited for; matrix products, arithmetic and copies ran while one was open for 7% of the time, Pallas kernels for 0%

commit v1 on v0

v1 whole, which is shorter than its diff:
```python
import jax
import jax.numpy as jnp
from jax import lax
from jax.sharding import PartitionSpec as P

F32 = jnp.float32
BF16 = jnp.bfloat16
HIGH3 = lax.Precision.HIGH


def dot3(a, b, ca=1, cb=0):
    return lax.dot_general(
        a, b, (((ca,), (cb,)), ((), ())), precision=HIGH3, preferred_element_type=F32
    )


def bdot(a, b):
    return lax.dot_general(
        a, b, (((2,), (1,)), ((0,), (0,))), precision=HIGH3, preferred_element_type=F32
    )


def inverse_pair(tiles):
    tile = tiles.shape[-1]
    rows = lax.broadcasted_iota(jnp.int32, (tile, tile), 0)
    cols = lax.broadcasted_iota(jnp.int32, (tile, tile), 1)
    eye = (rows == cols).astype(F32)
    recip = 1.0 / jnp.sum(tiles * eye, axis=2)
    inv = eye * recip[:, None, :]
    size = 1
    while size < tile:
        off = (rows // size % 2 == 1) & (cols // size == rows // size - 1)
        part = jnp.where(off, tiles, 0.0)
        if size == 1:
            inv = inv - recip[:, :, None] * part * recip[:, None, :]
        else:
            inv = inv - bdot(inv, bdot(part, inv))
        size *= 2
    return inv


def per_device(l_saved, l_grad):
    rows_here, tile = l_saved.shape[0], l_saved.shape[2]
    n_row = lax.axis_size("row")
    n_col = lax.axis_size("col")
    factor = l_saved.reshape(rows_here, tile, tile)
    grad = l_grad.reshape(rows_here, tile, tile)
    my_row = lax.axis_index("row")
    my_col = lax.axis_index("col")
    assert n_col % n_row == 0
    first = n_col // n_row
    loc = first - 1
    lo, hi = n_col - 2, n_col - 1

    l_dk = lax.all_gather(factor[loc], "row")[n_row - 2 :].reshape(2 * tile, tile)
    mine = jnp.concatenate([l_dk, grad[first:].reshape(-1, tile)], 0)
    zero = jnp.zeros_like(mine)
    both = jnp.concatenate(
        [jnp.where(my_col == lo, mine, zero), jnp.where(my_col == hi, mine, zero)], 1
    )
    both = lax.psum(both, "col")
    l_dd = both[: 2 * tile].astype(F32)
    g_d = both[2 * tile :]

    l66, l76, l77 = l_dd[:tile, :tile], l_dd[tile:, :tile], l_dd[tile:, tile:]
    inv = inverse_pair(jnp.stack([l66, l77]))
    w76 = -dot3(inv[1], dot3(l76, inv[0]))
    w = jnp.concatenate(
        [
            jnp.concatenate([inv[0], jnp.zeros_like(w76)], 1),
            jnp.concatenate([w76, inv[1]], 1),
        ],
        0,
    )

    below_l = factor[first:].reshape(-1, tile)
    h = lax.dot_general(g_d, below_l, (((0,), (0,)), ((), ())), preferred_element_type=F32)
    t = dot3(w, lax.psum(h, "row"), 0, 0)

    fresh = grad[loc].astype(F32)
    g_dk = lax.all_gather(grad[loc], "row")[n_row - 2 :].reshape(2 * tile, tile).astype(F32)
    q_mine = g_dk - t
    z2 = jnp.zeros_like(q_mine)
    q = lax.psum(
        jnp.concatenate([jnp.where(my_col == lo, q_mine, z2), jnp.where(my_col == hi, q_mine, z2)], 1),
        "col",
    )
    eye2 = jnp.eye(2 * tile, dtype=F32)
    q = jnp.tril(q)
    m = dot3(l_dd, q, 0, 0)
    phi = jnp.tril(m) - 0.5 * m * eye2
    half = dot3(dot3(w, phi, 0, 0), w)
    s = half + half.T
    out_dd = jnp.tril(s) - 0.5 * s * eye2

    right = my_col >= lo
    w_mine = jnp.where(my_col == lo, w[:, :tile], w[:, tile:])
    x = jnp.where(right, -w_mine, dot3(w, l_dk.astype(F32)))
    x_hi = lax.reduce_precision(x, 8, 7)
    x_lo = (x - x_hi).astype(BF16)
    x_hi = x_hi.astype(BF16)
    prod = jnp.dot(g_d, x_hi, preferred_element_type=F32) + jnp.dot(
        g_d, x_lo, preferred_element_type=F32
    )
    base = jnp.where(right, jnp.zeros((), BF16), grad[first:]).astype(F32)
    low = base - prod.reshape(-1, tile, tile)

    at_lo = my_row == n_row - 2
    s_row = jnp.where(at_lo, s[:tile], s[tile:])
    t_row = jnp.where(at_lo, t[:tile], t[tile:])
    own = fresh - (t_row + dot3(s_row, l_dk.astype(F32)))
    d_row = jnp.where(at_lo, out_dd[:tile], out_dd[tile:])
    d_own = jnp.where(my_col == lo, d_row[:, :tile], d_row[:, tile:])
    in_panel = my_row >= n_row - 2
    zt = jnp.zeros_like(fresh)
    own = jnp.where(
        in_panel, jnp.where(right, d_own, own), jnp.where(right, zt, fresh)
    )
    upper = jnp.where(right, jnp.zeros((), BF16), grad[:loc]).astype(F32)
    out = jnp.concatenate([upper, own[None], low], 0)
    return out.reshape(l_grad.shape)


def solution(mesh):
    spec = P(None, "row", None, "col", None)
    return jax.shard_map(
        per_device, mesh=mesh, in_specs=(spec, spec), out_specs=spec, check_vma=False
    )
```

time: 616 us -> 324 us (0.53); the launches traced: 608 us -> 324 us
  waiting for transfers between devices: 427 us -> 248 us
  other arithmetic: 73.2 us -> 12.1 us
  matrix products: 47.7 us -> 22.3 us
  local copies, waits for them, and re-layouts: 31.8 us -> 11.3 us
  blocking collectives: 0 us -> 15.9 us
  starting transfers between devices: 13.6 us -> 0.27 us
    psum x7 -> x3, waiting for transfers between devices: 427 us -> 248 us  [the longest x1 145 us: per_device(): both = lax.psum(both, 'col')]
    another operation x6 -> x0, other arithmetic: 41.1 us -> none  [right_solve(): return lax.linalg.triangular_solve(factor, rhs, left_side=False, lower=True)]
    select_n x5 -> x2, other arithmetic: 20.8 us -> 0.75 us  [the longest x1 0.67 us: per_device(): jnp.where(my_col == lo, mine, zero)]
    dot_general x12 -> x25, matrix products: 42.2 us -> 22.3 us  [the longest x8 10.1 us: dot3(): lax.dot_general(a, b, (((ca,), (cb,)), ((), ())), precision=HIGH3, prefer...]
    all_gather x0 -> x2, blocking collectives: none -> 15.9 us  [the longest x1 8.68 us: per_device(): lax.all_gather(factor[loc], 'row')[n_row - 2:].reshape(2 * tile, tile)]
    psum x7 -> x3, starting transfers between devices: 13.6 us -> 0.27 us  [the longest x1 0.22 us: per_device(): lax.psum(jnp.concatenate([jnp.where(my_col == lo, q_mine, z2), jnp.where(...]
    another operation x17 -> x1, local copies, waits for them, and re-layouts: 9.28 us -> 0.04 us  [per_device(): inv = inverse_pair(jnp.stack([l66, l77]))]
    reshape x2 -> x1, local copies, waits for them, and re-layouts: 12.1 us -> 3.88 us  [per_device(): return out.reshape(l_grad.shape)]
  transfers between devices with their start and end apart: 7 -> 3, of which waited for: 7 -> 3; matrix products, arithmetic and copies ran while one was open for 7% -> 3% of each run, Pallas kernels for 0% -> 0%
where the time goes in v1:
time: 324 us
  waiting for transfers between devices  248 us (77%)
  matrix products  22.3 us (7%)
  blocking collectives  15.9 us (5%)
  between operations  13.6 us (4%)
  other arithmetic  12.1 us (4%)
  local copies, waits for them, and re-layouts  11.3 us (3%)
    psum x1, waiting for transfers between devices, per_device(): both = lax.psum(both, 'col')  145 us
    psum x1, waiting for transfers between devices, per_device(): lax.psum(jnp.concatenate([jnp.where(my_col == lo, q_mine, z2), jnp.where(...  71.8 us
    psum x1, waiting for transfers between devices, per_device(): t = dot3(w, lax.psum(h, 'row'), 0, 0)  30.8 us
    dot_general x8, matrix products, dot3(): lax.dot_general(a, b, (((ca,), (cb,)), ((), ())), precision=HIGH3, prefer...  10.1 us
    all_gather x1, blocking collectives, per_device(): lax.all_gather(factor[loc], 'row')[n_row - 2:].reshape(2 * tile, tile)  8.68 us
    all_gather x1, blocking collectives, per_device(): lax.all_gather(grad[loc], 'row')[n_row - 2:].reshape(2 * tile, tile)  7.26 us
  transfers between devices with their start and end apart: 3, of which 3 were waited for; matrix products, arithmetic and copies ran while one was open for 3% of the time, Pallas kernels for 0%

profile of v1, /device:TPU:0, one launch (start us, length us, event | category | flops | bytes accessed | tf_op | source)
XLA Modules:
  0.0 323.6 jit_solution(8879946724786427271)
XLA Ops:
  6.5 0.9 slice.87
  7.5 8.7 %all-gather = bf16[4,1,256,1,256]{4,2,3,1,0:T(8,128)(2,1)S(1)} all-gather(bf16[1,1,256,1,256]{4,2,3,1,0:T(8,128)(2,1)S(1)} %slice.87), channel_id=2, replica_groups=mesh['row'=4,'col'=8] {'row'}, dimensions={0}, use_global_device_ids=true | all-gather | bytes 655360 | tf_op jit(solution)/shard_map/all_gather | solution.py:55
  16.2 1.7 slice.115
  18.6 2.3 pad_maximum_fusion
  21.0 1.5 copy-done.3
  23.2 7.3 %all-gather.1 = bf16[4,1,256,1,256]{4,2,3,1,0:T(8,128)(2,1)S(1)} all-gather(bf16[1,1,256,1,256]{4,2,3,1,0:T(8,128)(2,1)S(1)} %get-tuple-element.8), channel_id=3, replica_groups=mesh['row'=4,'col'=8] {'row'}, dimensions={0}, use_global_device_ids=true | all-gather | bytes 655360 | tf_op jit(solution)/shard_map/all_gather | solution.py:81
  30.5 0.7 slice.122
  32.9 145.4 %all-reduce.5.cloned.1.call-done = bf16[4096,512]{1,0:T(8,128)(2,1)} async-done(((bf16[4096,512]{1,0:T(8,128)(2,1)}), bf16[4096,512]{1,0:T(8,128)(2,1)}) %all-reduce.5.cloned.1.call-update) | async-done | bytes 4194320 | tf_op jit(solution)/shard_map/psum | solution.py:61
  178.3 1.2 slice_convert_fusion
  186.8 1.9 fusion.3
  189.1 1.4 convolution_select_fusion
  190.5 30.8 %all-reduce.7.cloned.1.call-done = f32[512,256]{1,0:T(8,128)} async-done(((f32[512,256]{1,0:T(8,128)}), f32[512,256]{1,0:T(8,128)}) %all-reduce.7.cloned.1.call-update) | async-done | bytes 524304 | tf_op jit(solution)/shard_map/psum | solution.py:78
  221.3 2.7 fusion.40
  224.0 1.2 pad_maximum_fusion.3
  225.2 3.3 %fusion.1 = f32[3584,256]{1,0:T(8,128)S(1)} fusion(bf16[4096,512]{1,0:T(8,128)(2,1)} %all-reduce.5.cloned.1.call-done, f32[512,256]{1,0:T(8,128)S(1)} %convolution_select_fusion), kind=kOutput, calls=%fused_computation.5 | convolution fusion | flops 939786240 | bytes 7864320 | tf_op jit(solution)/shard_map/dot_general | solution.py:102
  228.5 1.1 convolution_add_fusion
  229.7 2.3 convert_subtract_fusion
  231.9 71.8 %all-reduce.9.cloned.1.call-done = f32[512,512]{1,0:T(8,128)} async-done(((f32[512,512]{1,0:T(8,128)}), f32[512,512]{1,0:T(8,128)}) %all-reduce.9.cloned.1.call-update) | async-done | bytes 1048592 | tf_op jit(solution)/shard_map/psum | solution.py:84
  303.7 2.2 fusion.14
  305.9 1.0 fusion.9
  307.0 2.0 fusion.113
  309.0 1.3 copy.12
  310.3 1.6 select_subtract_fusion
  313.2 3.9 %reshape.79 = f32[16,1,256,1,256]{4,3,2,1,0:T(1,128)} reshape(f32[16,256,256]{2,1,0:T(8,128)S(1)} %pad_maximum_fusion.1) | data formatting | bytes 8388608 | tf_op jit(solution)/shard_map/reshape | solution.py:121
  (77 shorter events, 11.8 us)
Async XLA Ops:
  6.5 171.8 %all-reduce.5.cloned.1.call-start = ((), (), s32[]{:S(2)}) async-start(), calls=%async_computation | async-start | bytes 8388608 | tf_op jit(solution)/shard_map/psum | solution.py:61
  16.2 2.4 copy-start.6
  20.9 1.6 copy-start.3
  20.9 200.4 %all-reduce.7.cloned.1.call-start = ((), (), s32[]{:S(2)}) async-start(), calls=%async_computation.1 | async-start | bytes 1048576 | tf_op jit(solution)/shard_map/psum | solution.py:78
  183.9 2.2 copy-start
  184.3 2.5 slice-start
  186.1 119.8 %copy-start.4 = (f32[256,256]{1,0:T(8,128)}, f32[256,256]{1,0:T(8,128)S(1)}, u32[]{:S(2)}) copy-start(f32[256,256]{1,0:T(8,128)S(1)} %get-tuple-element.15) | copy-start | bytes 786436
  186.1 119.8 %copy-start.5 = (f32[256,256]{1,0:T(8,128)}, f32[256,256]{1,0:T(8,128)S(1)}, u32[]{:S(2)}) copy-start(f32[256,256]{1,0:T(8,128)S(1)} %get-tuple-element.16) | copy-start | bytes 786436
  188.8 115.0 %all-reduce.9.cloned.1.call-start = ((), (), s32[]{:S(2)}) async-start(), calls=%async_computation.2 | async-start | bytes 2097152 | tf_op jit(solution)/shard_map/psum | solution.py:84
  225.2 3.3 %copy-start.1 = (bf16[4096,512]{1,0:T(8,128)(2,1)S(1)}, bf16[4096,512]{1,0:T(8,128)(2,1)}, u32[]{:S(2)}) copy-start(bf16[4096,512]{1,0:T(8,128)(2,1)} %all-reduce.5.cloned.1.call-done) | copy-start | bytes 12582916
  309.0 3.1 copy-start.7
  310.3 1.7 copy-start.9
  310.3 2.5 copy-start.2
  310.3 2.5 copy-start.8
Sparse Core Ops, SparseCore 0:
  21.1 157.1 all-reduce.4
  188.9 32.3 all-reduce.6
  225.3 78.3 all-reduce.8

commit v2 on v1

--- a/solution.py
+++ b/solution.py
@@ -1,6 +1,10 @@
+import functools
+
 import jax
 import jax.numpy as jnp
 from jax import lax
+from jax.experimental import pallas as pl
+from jax.experimental.pallas import tpu as pltpu
 from jax.sharding import PartitionSpec as P
 
 F32 = jnp.float32
@@ -39,6 +43,134 @@
     return inv
 
 
+def spread_kernel(n_col, in_ref, out_ref, send_sem, recv_sem):
+    n = in_ref.shape[0]
+    ring = n_col // 2
+    col = lax.axis_index("col")
+    q, p = col // 2, col % 2
+    up = lax.rem(q + 1, ring) * 2 + p
+    down = lax.rem(q + ring - 1, ring) * 2 + p
+    twin = 2 * q + 1 - p
+
+    barrier = pltpu.get_barrier_semaphore()
+    for peer in (up, down, twin):
+        pl.semaphore_signal(barrier, inc=1, device_id={"col": peer}, device_id_type=pl.DeviceIdType.MESH)
+    pl.semaphore_wait(barrier, 3)
+
+    k_of = (lax.rem(q + 1, ring), ring - 1 - q)
+    nexts = (up, down)
+    backs = (down, up)
+    streams = [(s, d) for s in (0, 1) for d in (0, 1)]
+
+    def copy(src, s, t, slot, dev):
+        return pltpu.make_async_remote_copy(
+            src_ref=src.at[t],
+            dst_ref=out_ref.at[s, t],
+            send_sem=send_sem.at[s, t, slot],
+            recv_sem=recv_sem.at[s, t],
+            device_id={"col": dev},
+            device_id_type=pl.DeviceIdType.MESH,
+        )
+
+    def roles(s, d, idx):
+        k = k_of[d]
+        main = p == s
+        once = idx % 3 == 0
+        source = main & (k == 0)
+        fwd = (main | once) & (k < ring - 1)
+        cross = main & jnp.where(once, k == 0, k > 0)
+        back = jnp.logical_not(once) & jnp.logical_not(main) & (k == 1)
+        return source, fwd, cross, back
+
+    half = (n + 1) // 2
+
+    def step(j, _):
+        for s, d in streams:
+            lag = k_of[d] + jnp.where(p == s, 0, 1)
+            idx = j - lag
+            t = 2 * idx + d
+            live = (idx >= 0) & (t < n)
+            source, fwd, cross, back = roles(s, d, idx)
+            moves = fwd | cross | back
+
+            @pl.when(live & source)
+            def _():
+                @pl.when(fwd)
+                def _():
+                    copy(in_ref, s, t, 0, nexts[d]).start()
+
+                @pl.when(cross)
+                def _():
+                    copy(in_ref, s, t, 1, twin).start()
+
+            @pl.when(live & moves & jnp.logical_not(source))
+            def _():
+                copy(out_ref.at[s], s, t, 0, twin).wait_recv()
+
+                @pl.when(fwd)
+                def _():
+                    copy(out_ref.at[s], s, t, 0, nexts[d]).start()
+
+                @pl.when(cross)
+                def _():
+                    copy(out_ref.at[s], s, t, 1, twin).start()
+
+                @pl.when(back)
+                def _():
+                    copy(out_ref.at[s], s, t, 0, backs[d]).start()
+
+        return 0
+
+    lax.fori_loop(0, half + ring + 1, step, 0)
+
+    for s in (0, 1):
+
+        @pl.when(col == n_col - 2 + s)
+        def _():
+            def keep(t, _):
+                out_ref[s, t] = in_ref[t]
+                return 0
+
+            lax.fori_loop(0, n, keep, 0)
+
+    def finish(idx, _):
+        for s, d in streams:
+            t = 2 * idx + d
+            live = t < n
+            source, fwd, cross, back = roles(s, d, idx)
+            moves = fwd | cross | back
+
+            @pl.when(live & jnp.logical_not(moves) & jnp.logical_not(source))
+            def _():
+                copy(out_ref.at[s], s, t, 0, twin).wait_recv()
+
+            @pl.when(live & (fwd | back))
+            def _():
+                copy(out_ref.at[s], s, t, 0, twin).wait_send()
+
+            @pl.when(live & cross)
+            def _():
+                copy(out_ref.at[s], s, t, 1, twin).wait_send()
+
+        return 0
+
+    lax.fori_loop(0, half, finish, 0)
+
+
+def spread(mine, n_col):
+    n, tile = mine.shape[0], mine.shape[1]
+    vmem = pl.BlockSpec(memory_space=pltpu.VMEM)
+    return pl.pallas_call(
+        functools.partial(spread_kernel, n_col),
+        out_shape=jax.ShapeDtypeStruct((2, n, tile, tile), mine.dtype),
+        in_specs=[vmem],
+        out_specs=vmem,
+        scratch_shapes=[pltpu.SemaphoreType.DMA((2, n, 2)), pltpu.SemaphoreType.DMA((2, n))],
+        compiler_params=pltpu.CompilerParams(collective_id=0, has_side_effects=True),
+        name="spread",
+    )(mine)
+
+
 def per_device(l_saved, l_grad):
     rows_here, tile = l_saved.shape[0], l_saved.shape[2]
     n_row = lax.axis_size("row")
@@ -52,15 +184,12 @@
     loc = first - 1
     lo, hi = n_col - 2, n_col - 1
 
-    l_dk = lax.all_gather(factor[loc], "row")[n_row - 2 :].reshape(2 * tile, tile)
-    mine = jnp.concatenate([l_dk, grad[first:].reshape(-1, tile)], 0)
-    zero = jnp.zeros_like(mine)
-    both = jnp.concatenate(
-        [jnp.where(my_col == lo, mine, zero), jnp.where(my_col == hi, mine, zero)], 1
-    )
-    both = lax.psum(both, "col")
-    l_dd = both[: 2 * tile].astype(F32)
-    g_d = both[2 * tile :]
+    l_rows = lax.all_gather(factor[loc], "row")[n_row - 2 :]
+    l_dk = l_rows.reshape(2 * tile, tile)
+    both = spread(jnp.concatenate([l_rows, grad[first:]], 0), n_col)
+    l_dd = jnp.concatenate([both[i, :2].reshape(2 * tile, tile) for i in (0, 1)], 1).astype(F32)
+    g_lo = both[0, 2:].reshape(-1, tile)
+    g_hi = both[1, 2:].reshape(-1, tile)
 
     l66, l76, l77 = l_dd[:tile, :tile], l_dd[tile:, :tile], l_dd[tile:, tile:]
     inv = inverse_pair(jnp.stack([l66, l77]))
@@ -74,7 +203,13 @@
     )
 
     below_l = factor[first:].reshape(-1, tile)
-    h = lax.dot_general(g_d, below_l, (((0,), (0,)), ((), ())), preferred_element_type=F32)
+    h = jnp.concatenate(
+        [
+            lax.dot_general(g, below_l, (((0,), (0,)), ((), ())), preferred_element_type=F32)
+            for g in (g_lo, g_hi)
+        ],
+        0,
+    )
     t = dot3(w, lax.psum(h, "row"), 0, 0)
 
     fresh = grad[loc].astype(F32)
@@ -99,8 +234,10 @@
     x_hi = lax.reduce_precision(x, 8, 7)
     x_lo = (x - x_hi).astype(BF16)
     x_hi = x_hi.astype(BF16)
-    prod = jnp.dot(g_d, x_hi, preferred_element_type=F32) + jnp.dot(
-        g_d, x_lo, preferred_element_type=F32
+    prod = sum(
+        jnp.dot(g, part[i * tile : (i + 1) * tile], preferred_element_type=F32)
+        for part in (x_lo, x_hi)
+        for i, g in enumerate((g_lo, g_hi))
     )
     base = jnp.where(right, jnp.zeros((), BF16), grad[first:]).astype(F32)
     low = base - prod.reshape(-1, tile, tile)

time: 324 us -> 245 us (0.76)
  waiting for transfers between devices: 248 us -> 72.7 us
  Pallas kernels: 0 us -> 83.1 us
  matrix products: 22.3 us -> 29.8 us
  local copies, waits for them, and re-layouts: 11.3 us -> 18 us
    psum x1 -> x0, waiting for transfers between devices: 145 us -> none  [per_device(): both = lax.psum(both, 'col')]
    pallas_call x0 -> x1, Pallas kernels: none -> 83.1 us  [spread(): pl.pallas_call(functools.partial(spread_kernel, n_col), out_shape=jax.Sha...]
    psum x1, waiting for transfers between devices: 30.8 us -> 4.54 us  [per_device(): t = dot3(w, lax.psum(h, 'row'), 0, 0)]
    dot_general x3 -> x6, matrix products: 6.37 us -> 12.7 us  [the longest x4 11.3 us: per_device(): jnp.dot(g, part[i * tile:(i + 1) * tile], preferred_element_type=F32)]
    psum x1, waiting for transfers between devices: 71.8 us -> 68.1 us  [per_device(): lax.psum(jnp.concatenate([jnp.where(my_col == lo, q_mine, z2), jnp.where(...]
  transfers between devices with their start and end apart: 3 -> 2, of which waited for: 3 -> 2; matrix products, arithmetic and copies ran while one was open for 3% -> 12% of each run, Pallas kernels for 0% -> 0%
where the time goes in v2:
time: 245 us
  Pallas kernels  83.1 us (34%)
  waiting for transfers between devices  72.7 us (30%)
  matrix products  29.8 us (12%)
  local copies, waits for them, and re-layouts  18 us (7%)
  blocking collectives  15.6 us (6%)
  between operations  14 us (6%)
  other arithmetic  11.4 us (5%)
    pallas_call x1, Pallas kernels, spread(): pl.pallas_call(functools.partial(spread_kernel, n_col), out_shape=jax.Sha...  83.1 us
    psum x1, waiting for transfers between devices, per_device(): lax.psum(jnp.concatenate([jnp.where(my_col == lo, q_mine, z2), jnp.where(...  68.1 us
    dot_general x8, matrix products, dot3(): lax.dot_general(a, b, (((ca,), (cb,)), ((), ())), precision=HIGH3, prefer...  11.4 us
    dot_general x4, matrix products, per_device(): jnp.dot(g, part[i * tile:(i + 1) * tile], preferred_element_type=F32)  11.3 us
    all_gather x1, blocking collectives, per_device(): l_rows = lax.all_gather(factor[loc], 'row')[n_row - 2:]  8.66 us
    all_gather x1, blocking collectives, per_device(): lax.all_gather(grad[loc], 'row')[n_row - 2:].reshape(2 * tile, tile)  6.92 us
    reshape x1, local copies, waits for them, and re-layouts, per_device(): return out.reshape(l_grad.shape)  6.33 us
    dot_general x14, matrix products, bdot(): lax.dot_general(a, b, (((2,), (1,)), ((0,), (0,))), precision=HIGH3, pref...  5.75 us
  transfers between devices with their start and end apart: 2, of which 2 were waited for; matrix products, arithmetic and copies ran while one was open for 12% of the time, Pallas kernels for 0%

profile of v2, /device:TPU:0, one launch (start us, length us, event | category | flops | bytes accessed | tf_op | source)
XLA Modules:
  0.0 244.6 jit_solution(17539181726368961872)
XLA Ops:
  6.5 3.0 %slice.128 = bf16[14,1,256,1,256]{4,2,3,1,0:T(8,128)(2,1)} slice(bf16[16,1,256,1,256]{4,2,3,1,0:T(8,128)(2,1)} %param.2), slice={[2:16], [0:1], [0:256], [0:1], [0:256]} | slice | bytes 3670016 | tf_op jit(solution)/shard_map/slice | solution.py:205
  10.5 8.7 %all-gather = bf16[4,1,256,1,256]{4,2,3,1,0:T(8,128)(2,1)S(1)} all-gather(bf16[1,1,256,1,256]{4,2,3,1,0:T(8,128)(2,1)S(1)} %slice-done), channel_id=2, replica_groups=mesh['row'=4,'col'=8] {'row'}, dimensions={0}, use_global_device_ids=true | all-gather | bytes 655360 | tf_op jit(solution)/shard_map/all_gather | solution.py:187
  19.2 1.5 pad_maximum_fusion.in_ref
  20.7 83.1 %spread.1 = bf16[2,16,256,256]{3,2,1,0:T(8,128)(2,1)} custom-call(bf16[16,256,256]{2,1,0:T(8,128)(2,1)} %pad_maximum_fusion.in_ref), custom_call_target="tpu_custom_call" | custom-call | tf_op jit(solution)/shard_map/spread/pallas_call | solution.py:163
  103.8 2.5 %fusion.116 = (bf16[1,14,256,256]{3,2,1,0:T(8,128)(2,1)S(1)}, bf16[1,14,256,256]{3,2,1,0:T(8,128)(2,1)S(1)}) fusion(bf16[2,16,256,256]{3,2,1,0:T(8,128)(2,1)} %spread.1), kind=kLoop, calls=%fused_computation.236 | loop fusion | bytes 7340032 | tf_op jit(solution)/shard_map/slice | solution.py:192
  109.1 1.1 fusion.117
  118.6 1.8 fusion.98
  120.5 1.4 convolution_negate_fusion
  122.0 1.7 bitcast_convert_fusion
  123.7 6.9 %all-gather.1 = bf16[4,1,256,1,256]{4,2,3,1,0:T(8,128)(2,1)S(1)} all-gather(bf16[1,1,256,1,256]{4,2,3,1,0:T(8,128)(2,1)S(1)} %get-tuple-element.12), channel_id=3, replica_groups=mesh['row'=4,'col'=8] {'row'}, dimensions={0}, use_global_device_ids=true | all-gather | bytes 655360 | tf_op jit(solution)/shard_map/all_gather | solution.py:216
  130.7 1.2 reduce-precision_convert_fusion
  133.4 2.5 %convolution_add_fusion.2 = f32[3584,256]{1,0:T(8,128)} fusion(f32[3584,256]{1,0:T(8,128)S(1)} %fusion.96, bf16[3584,256]{1,0:T(8,128)(2,1)S(1)} %bitcast.83, bf16[512,256]{1,0:T(8,128)(2,1)S(1)} %get-tuple-element.18), kind=kOutput, calls=%fused_computation.2 | convolution fusion | flops 470679552 | bytes 9306112 | tf_op jit(solution)/shard_map/dot_general | solution.py:238
  135.9 4.5 %all-reduce.4.cloned.1.call-done = f32[512,256]{1,0:T(8,128)} async-done(((f32[512,256]{1,0:T(8,128)}), f32[512,256]{1,0:T(8,128)}) %all-reduce.4.cloned.1.call-update) | async-done | bytes 524304 | tf_op jit(solution)/shard_map/psum | solution.py:213
  140.4 2.7 %fusion.34 = (f32[512,256]{1,0:T(8,128)S(1)}, f32[512,256]{1,0:T(8,128)S(1)}, f32[512,256]{1,0:T(8,128)}) fusion(bf16[2,1,256,1,256]{4,2,3,1,0:T(8,128)(2,1)S(1)} %slice-done.1, pred[]{:T(512)S(6)} %eq.82, pred[]{:T(512)S(6)} %eq.101, f32[512,256]{1,0:T(8,128)} %all-reduce.4.cloned.1.call-done, f32[256,256]{1,0:T(8,128)S(1)} %get-tuple-element.22, ...), kind=kOutput, calls=%fused_computation.114 | convolution fusion | flops 404226048 | bytes 3145730 | tf_op jit(solution)/shard_map/dot_general | solution.py:16
  143.1 1.1 pad_maximum_fusion.1
  144.2 4.5 %convolution_add_fusion.1 = f32[3584,256]{1,0:T(8,128)} fusion(f32[3584,256]{1,0:T(8,128)} %convolution_add_fusion.2, bf16[3584,256]{1,0:T(8,128)(2,1)S(1)} %bitcast.80, bf16[512,256]{1,0:T(8,128)(2,1)S(1)} %copy-done.17), kind=kOutput, calls=%fused_computation.1 | convolution fusion | flops 470679552 | bytes 9306112 | tf_op jit(solution)/shard_map/dot_general | solution.py:238
  148.7 3.7 %convolution_add_fusion = f32[3584,256]{1,0:T(8,128)S(1)} fusion(f32[3584,256]{1,0:T(8,128)} %convolution_add_fusion.1, bf16[3584,256]{1,0:T(8,128)(2,1)} %bitcast.82, bf16[512,256]{1,0:T(8,128)(2,1)} %get-tuple-element.17), kind=kOutput, calls=%fused_computation | convolution fusion | flops 470679552 | bytes 9306112 | tf_op jit(solution)/shard_map/dot_general | solution.py:238
  152.5 2.3 convert_subtract_fusion
  154.7 68.1 %all-reduce.6.cloned.1.call-done = f32[512,512]{1,0:T(8,128)} async-done(((f32[512,512]{1,0:T(8,128)}), f32[512,512]{1,0:T(8,128)}) %all-reduce.6.cloned.1.call-update) | async-done | bytes 1048592 | tf_op jit(solution)/shard_map/psum | solution.py:219
  222.8 2.0 fusion.9
  224.9 1.0 fusion.4
  226.9 1.3 copy.15
  228.2 1.6 select_subtract_fusion
  231.5 6.3 %copy.18 = f32[16,1,256,1,256]{4,3,2,1,0:T(1,128)} copy(f32[16,1,256,1,256]{4,2,0,3,1:T(8,128)S(1)} %maximum_bitcast_fusion) | data formatting | bytes 8388608 | tf_op jit(solution)/shard_map/reshape | solution.py:258
  (104 shorter events, 16.1 us)
Async XLA Ops:
  6.5 3.0 %copy-start.3 = (bf16[16,1,256,1,256]{4,2,3,1,0:T(8,128)(2,1)S(1)}, bf16[16,1,256,1,256]{4,2,3,1,0:T(8,128)(2,1)}, u32[]{:S(2)}) copy-start(bf16[16,1,256,1,256]{4,2,3,1,0:T(8,128)(2,1)} %param.3) | copy-start | bytes 6291460
  6.5 133.9 %all-reduce.4.cloned.1.call-start = ((), (), s32[]{:S(2)}) async-start(), calls=%async_computation | async-start | bytes 1048576 | tf_op jit(solution)/shard_map/psum | solution.py:213
  9.6 0.9 slice-start
  19.2 111.5 %copy-start.18 = (bf16[2,1,256,1,256]{4,2,0,3,1:T(8,128)(2,1)}, bf16[2,1,256,1,256]{4,2,0,3,1:T(8,128)(2,1)S(1)}, u32[]{:S(2)}) copy-start(bf16[2,1,256,1,256]{4,2,0,3,1:T(8,128)(2,1)S(1)} %get-tuple-element.19) | copy-start | bytes 786436
  103.8 2.6 %copy-start.15 = (bf16[14,1,256,1,256]{4,2,3,1,0:T(8,128)(2,1)S(1)}, bf16[14,1,256,1,256]{4,2,3,1,0:T(8,128)(2,1)}, u32[]{:S(2)}) copy-start(bf16[14,1,256,1,256]{4,2,3,1,0:T(8,128)(2,1)} %slice.128) | copy-start | bytes 5505028
  106.3 1.3 copy-start
  109.1 113.7 %all-reduce.6.cloned.1.call-start = ((), (), s32[]{:S(2)}) async-start(), calls=%async_computation.1 | async-start | bytes 2097152 | tf_op jit(solution)/shard_map/psum | solution.py:219
  120.5 19.9 %copy-start.5 = (f32[256,256]{1,0:T(8,128)}, f32[256,256]{1,0:T(8,128)S(1)}, u32[]{:S(2)}) copy-start(f32[256,256]{1,0:T(8,128)S(1)} %get-tuple-element.21) | copy-start | bytes 786436
  120.5 19.9 %copy-start.8 = (f32[256,256]{1,0:T(8,128)}, f32[256,256]{1,0:T(8,128)S(1)}, u32[]{:S(2)}) copy-start(f32[256,256]{1,0:T(8,128)S(1)} %get-tuple-element.22) | copy-start | bytes 786436
  130.6 1.3 copy-start.16
  131.9 1.5 copy-start.1
  133.4 7.0 %slice-start.1 = ((bf16[4,1,256,1,256]{4,2,3,1,0:T(8,128)(2,1)}), bf16[2,1,256,1,256]{4,2,3,1,0:T(8,128)(2,1)S(1)}, s32[]{:S(2)}) async-start(bf16[4,1,256,1,256]{4,2,3,1,0:T(8,128)(2,1)} %copy-done.16), calls=%async_computation.3 | async-start | bytes 524288 | tf_op jit(solution)/shard_map/slice | solution.py:216
  143.1 1.2 copy-start.17
  148.7 3.7 %copy-start.4 = (bf16[16,1,256,1,256]{4,2,3,1,0:T(8,128)(2,1)S(1)}, bf16[16,1,256,1,256]{4,2,3,1,0:T(8,128)(2,1)}, u32[]{:S(2)}) copy-start(bf16[16,1,256,1,256]{4,2,3,1,0:T(8,128)(2,1)} %param.3) | copy-start | bytes 6291460
  152.4 70.4 %copy-start.12 = (bf16[1,2,256,256]{3,2,1,0:T(8,128)(2,1)S(1)}, bf16[1,2,256,256]{3,2,1,0:T(8,128)(2,1)}, u32[]{:S(2)}) copy-start(bf16[1,2,256,256]{3,2,1,0:T(8,128)(2,1)} %copy-done.11) | copy-start | bytes 786436
  152.5 70.4 %copy-start.14 = (bf16[1,2,256,256]{3,2,1,0:T(8,128)(2,1)S(1)}, bf16[1,2,256,256]{3,2,1,0:T(8,128)(2,1)}, u32[]{:S(2)}) copy-start(bf16[1,2,256,256]{3,2,1,0:T(8,128)(2,1)} %copy-done.13) | copy-start | bytes 786436
  154.7 70.1 %copy-start.6 = (f32[256,256]{1,0:T(8,128)S(1)}, f32[256,256]{1,0:T(8,128)}, u32[]{:S(2)}) copy-start(f32[256,256]{1,0:T(8,128)} %copy-done.5) | copy-start | bytes 786436
  154.7 70.1 %copy-start.9 = (f32[256,256]{1,0:T(8,128)S(1)}, f32[256,256]{1,0:T(8,128)}, u32[]{:S(2)}) copy-start(f32[256,256]{1,0:T(8,128)} %copy-done.8) | copy-start | bytes 786436
  224.8 1.1 copy-start.7
  224.9 1.1 copy-start.10
  228.2 1.8 copy-start.19
  228.2 1.8 copy-start.21
  228.2 2.6 %copy-start.2 = (f32[14,256,256]{2,1,0:T(8,128)S(1)}, f32[14,256,256]{2,1,0:T(8,128)}, u32[]{:S(2)}) copy-start(f32[14,256,256]{2,1,0:T(8,128)} %convert_subtract_fusion) | copy-start | bytes 11010052
  229.9 1.2 copy-start.20
  (2 other events, 1.6 us)
Sparse Core Ops, SparseCore 0:
  109.2 31.1 all-reduce.3
  144.3 78.4 all-reduce.5
